TPU v7x, 256 devices: a 8x8x2 block of a 8x8x16 slice. The times are simulated.
256 devices in a mesh: groups: 2 (over z), expert: 128 (over y, x, core).
Axes of the slice: x: 8, y: 8, z: 2, core: 2. Of those that a mesh axis runs over, the one named last changes fastest.
The devices are a block of a 8x8x16 slice.
Arguments:
- tokens: bfloat16 [2048, 4096], P(('groups', 'expert')), parts along dimension 0, may hold values from -400 to 400
- norm_gain: float32 [4096], replicated, may hold values from 0.1 to 1.9
- expert_ids: int32 [2048, 8], P(('groups', 'expert')), parts along dimension 0, may hold values from 0 to 63, all different within a row; in each aligned block of 8 rows (0 to 7, 8 to 15, ...) at most 2 rows name the same one
- route_score: float32 [2048, 8], P(('groups', 'expert')), parts along dimension 0, may hold values from 0.05 to 1
- expert_pair: int32 [128], P('groups'), parts along dimension 0, may hold values from 0 to 63, each once
- w_in: bfloat16 [256, 4096, 768], P(('groups', 'expert')), parts along dimension 0, may hold values from -0.09375 to 0.09375
- w_out: bfloat16 [256, 384, 4096], P(('groups', 'expert')), parts along dimension 0, may hold values from -0.4375 to 0.4375
Outputs:
- mixed: bfloat16 [2048, 4096], P(('groups', 'expert')), parts along dimension 0
There are 2 independent parts, one for each index of `groups`. A program takes and returns all parts, laid end to end along the dimension named above; an argument that names none is the same for every part. Nothing has to cross between parts.
Inputs may be any that keep to these rules, and one draw needn't show every extreme that they name: `expert_ids`: each token names 8 different experts; among the tokens of one device no expert is named by more than 2 tokens, and in some devices' tokens one expert is named by exactly 2. `expert_pair`: each value once.
All inputs are finite; a program needn't handle non-finite values.
Results may differ from a plain program's by a relative error of at most 0.0076.
Values may be sent and summed in bfloat16 or wider, within the bound.
A program may use at most 64 MiB of HBM per device.

v0:
```python
import jax
import jax.numpy as jnp
from jax import lax
from jax.sharding import Mesh
from jax.sharding import PartitionSpec as P

EXPERT = ("expert_0", "expert_1", "expert_2")
GROUPS_EXPERT = ("groups", "expert_0", "expert_1", "expert_2")


def partner(block, axis, stride):
    count = lax.axis_size(axis)
    route = []
    for low in range(count):
        high = low | 1 << stride
        if high != low and high < count:
            route += [(low, high), (high, low)]
    return lax.ppermute(block, axis, route)


def cut_along(x, dim, length):
    lengths = x.shape
    tiles = x.reshape(*lengths[:dim], length, lengths[dim] // length, *lengths[dim + 1 :])
    return jnp.moveaxis(tiles, dim, 0)


def in_order(tiles, dim):
    tiles = jnp.moveaxis(tiles, 0, dim)
    lengths = tiles.shape
    return tiles.reshape(*lengths[:dim], lengths[dim] * lengths[dim + 1], *lengths[dim + 2 :])


def turned_blocks(tiles, axes, turns):
    lengths = [lax.axis_size(a) for a in axes]
    tiles = tiles.reshape(*lengths, *tiles.shape[1:])
    for k in turns:
        tiles = lax.all_to_all(tiles, axes[k], split_axis=k, concat_axis=k, tiled=True)
    return tiles.reshape(-1, *tiles.shape[len(axes) :])


def two_step_exchange(x, groups, turns, split_dim, concat_dim):
    length = lax.axis_size(groups[0]) * lax.axis_size(groups[1])
    tiles = cut_along(x, split_dim, length)
    return in_order(turned_blocks(tiles, groups, turns), concat_dim)


def on_device(tokens, norm_gain, expert_ids, route_score, expert_pair, w_in, w_out):
    devices = lax.axis_size(EXPERT)
    experts = devices // 2
    tok_rows, choices_each = expert_ids.shape
    width = tokens.shape[1]
    half_units = w_out.shape[1]
    capacity = min(tok_rows, (tok_rows * choices_each + experts - 1) // experts + 1)
    half_slots = (capacity + 1) // 2
    slots_each = 2 * half_slots
    widened = tokens.astype(jnp.float32)
    meansq = jnp.mean(widened * widened, axis=-1, keepdims=True)
    normed = (widened * lax.rsqrt(meansq + 1e-06) * norm_gain).astype(jnp.bfloat16)
    shares = (route_score / jnp.sum(route_score, axis=-1, keepdims=True)).astype(jnp.bfloat16)
    onehot = (expert_ids[:, :, None] == jnp.arange(experts, dtype=jnp.int32)).astype(jnp.int32)
    flattened = onehot.reshape(tok_rows * choices_each, experts)
    earlier = jnp.cumsum(flattened, axis=0) - flattened
    ranking = jnp.sum(earlier * flattened, axis=-1).reshape(tok_rows, choices_each)
    station = jnp.sum(onehot * expert_pair, axis=-1)
    source = lax.axis_index(EXPERT)
    member = (ranking + source) % 2
    slot_of = station * slots_each + member * half_slots + ranking // 2
    slot_key = jnp.arange(experts * slots_each, dtype=jnp.int32)
    matches = slot_of[:, :, None] == slot_key
    combine_weights = jnp.sum(
        jnp.where(matches, shares.astype(jnp.float32)[:, :, None], 0.0), axis=1
    ).astype(jnp.bfloat16)
    placing = jnp.any(matches, axis=1).astype(jnp.bfloat16)
    gathered = lax.dot_general(
        placing, normed, (((0,), (0,)), ((), ())), preferred_element_type=jnp.float32
    )
    gathered = gathered.astype(jnp.bfloat16)
    outgoing = gathered.reshape(devices, half_slots, width)
    arrived = two_step_exchange(outgoing, (("expert_0", "expert_1"), "expert_2"), (1, 0), 0, 0)
    slot_count = arrived.shape[1]
    partner_rows = partner(arrived, EXPERT, 0)
    both_rows = jnp.concatenate([arrived, partner_rows], axis=1)
    projected = jnp.dot(
        both_rows.reshape(devices * 2 * slot_count, width),
        w_in[0],
        preferred_element_type=jnp.float32,
    )
    hidden = (jax.nn.silu(projected[:, :half_units]) * projected[:, half_units:]).astype(
        jnp.bfloat16
    )
    partial_value = jnp.dot(hidden, w_out[0], preferred_element_type=jnp.float32)
    partial_value = partial_value.reshape(devices, 2 * slot_count, width)
    own_part = partial_value[:, :slot_count]
    other_part = partial_value[:, slot_count:]
    from_partner = partner(other_part.astype(jnp.bfloat16), EXPERT, 0).astype(other_part.dtype)
    finished = (own_part + from_partner).astype(jnp.bfloat16)
    returned = lax.all_to_all(finished, EXPERT, split_axis=0, concat_axis=0, tiled=True)
    outputs = returned.reshape(experts * slots_each, width)
    mixture = jnp.dot(combine_weights, outputs, preferred_element_type=jnp.float32)
    return mixture.astype(jnp.bfloat16)


def solution(mesh):
    split = Mesh(
        mesh.devices.reshape(mesh.shape["groups"], 8, 8, 2),
        ("groups", "expert_0", "expert_1", "expert_2"),
    )
    placed = (
        P(GROUPS_EXPERT, None),
        P(),
        P(GROUPS_EXPERT, None),
        P(GROUPS_EXPERT, None),
        P("groups"),
        P(GROUPS_EXPERT, None, None),
        P(GROUPS_EXPERT, None, None),
    )
    return jax.shard_map(
        on_device, mesh=split, in_specs=placed, out_specs=P(GROUPS_EXPERT, None), check_vma=False
    )
```

profile of v0, /device:TPU:514, one launch (start us, length us, event | category | flops | bytes accessed | tf_op | source)
XLA Modules:
  0.0 153.0 jit_solution(14705962155281947720)
XLA Ops:
  0.0 0.9 eq.40
  0.9 1.0 fusion.9
  2.0 1.0 select_reduce_fusion.2
  3.0 0.1 reduce_window_sum.11
  3.1 0.2 select_reduce_fusion.1
  3.5 2.3 %convolution_convert_fusion = bf16[128,4096]{1,0:T(8,128)(2,1)} fusion(pred[8,128]{1,0:T(8,128)(4,1)S(1)} %fusion.15, bf16[8,4096]{1,0:T(8,128)(2,1)} %param.7, f32[4096]{0:T(1024)} %param.8, f32[8]{0:T(128)S(1)} %add_rsqrt_fusion), kind=kOutput, calls=%fused_computation.2 | convolution fusion | flops 9043968 | bytes 1131552 | tf_op jit(solution)/shard_map/dot_general | solution.py:74
  5.8 2.5 %reshape_reshape_reshape.3 = bf16[64,2,1,1,4096]{4,1,0,3,2:T(2,128)(2,1)} reshape(bf16[128,4096]{1,0:T(8,128)(2,1)} %convolution_convert_fusion) | data formatting | bytes 2097152 | tf_op jit(solution)/shard_map/reshape;reshape;reshape | solution.py:35
  8.4 1.8 %copy.22 = bf16[64,2,1,1,4096]{4,0,3,2,1:T(8,128)(2,1)S(1)} copy(bf16[64,2,1,1,4096]{4,1,0,3,2:T(2,128)(2,1)} %reshape_reshape_reshape.3) | data formatting | bytes 2097152 | tf_op jit(solution)/shard_map/reshape;reshape;reshape | solution.py:35
  10.2 4.6 %all_to_all.15 = bf16[64,2,1,1,4096]{4,0,3,2,1:T(8,128)(2,1)S(1)} all-to-all(bf16[64,2,1,1,4096]{4,0,3,2,1:T(8,128)(2,1)S(1)} %copy.22), channel_id=1, replica_groups=mesh['groups'=2,'expert_0'=8,'expert_1'=8,'expert_2'=2] {'expert_2'}, dimensions={1} | all-to-all | bytes 2097152 | tf_op jit(solution)/shard_map/all_to_all | solution.py:37
  14.8 1.1 copy.23
  15.9 53.8 %all_to_all.16 = bf16[64,2,1,1,4096]{4,1,3,2,0:T(2,128)(2,1)} all-to-all(bf16[64,2,1,1,4096]{4,1,3,2,0:T(2,128)(2,1)S(1)} %copy.23), channel_id=1, replica_groups=mesh['groups'=2,'expert_0'=8,'expert_1'=8,'expert_2'=2] {'expert_0','exp..., dimensions={0} | all-to-all | bytes 2097152 | tf_op jit(solution)/shard_map/all_to_all | solution.py:37
  69.7 2.3 %reshape_reshape.3 = bf16[128,1,4096]{2,0,1:T(8,128)(2,1)} reshape(bf16[64,2,1,1,4096]{4,1,3,2,0:T(2,128)(2,1)} %all_to_all.16) | data formatting | bytes 2097152 | tf_op jit(solution)/shard_map/reshape;reshape | solution.py:30
  72.0 2.9 %collective-permute-done = bf16[128,1,4096]{2,0,1:T(8,128)(2,1)S(1)} collective-permute-done((bf16[128,1,4096]{2,0,1:T(8,128)(2,1)}, bf16[128,1,4096]{2,0,1:T(8,128)(2,1)S(1)}, u32[]{:S(2)}, u32[]{:S(2)}) %collective-permute-start) | collective-permute-done | bytes 1048608 | tf_op jit(solution)/shard_map/ppermute | solution.py:18
  74.8 1.4 pad_maximum_fusion
  76.2 3.5 %copy.24 = bf16[128,2,4096]{2,1,0:T(2,128)(2,1)} copy(bf16[128,2,4096]{2,0,1:T(8,128)(2,1)S(1)} %pad_maximum_fusion) | data formatting | bytes 4194304 | tf_op jit(solution)/shard_map/concatenate | solution.py:82
  79.8 4.1 %reshape.75 = bf16[256,4096]{1,0:T(8,128)(2,1)} reshape(bf16[128,2,4096]{2,1,0:T(2,128)(2,1)} %copy.24) | data formatting | bytes 4194304 | tf_op jit(solution)/shard_map/reshape | solution.py:84
  83.9 5.2 %fusion = f32[256,768]{1,0:T(8,128)S(1)} fusion(bf16[256,4096]{1,0:T(8,128)(2,1)} %reshape.75, bf16[1,4096,768]{2,1,0:T(8,128)(2,1)} %param.12), kind=kOutput, calls=%fused_computation | convolution fusion | flops 1610612736 | bytes 9175040 | tf_op jit(solution)/shard_map/dot_general | solution.py:83
  89.1 0.1 fusion.7
  89.4 1.2 fusion.2
  90.6 0.1 slice.29
  90.7 0.4 collective-permute-start.1
  91.2 2.5 %collective-permute-done.1 = bf16[128,1,4096]{2,0,1:T(8,128)(2,1)S(1)} collective-permute-done((bf16[128,1,4096]{2,0,1:T(8,128)(2,1)S(1)}, bf16[128,1,4096]{2,0,1:T(8,128)(2,1)S(1)}, u32[]{:S(2)}, u32[]{:S(2)}) %collective-permute-start.1) | collective-permute-done | bytes 1048608 | tf_op jit(solution)/shard_map/ppermute | solution.py:18
  93.7 1.2 fusion.4
  94.9 0.5 broadcast.105
  95.5 3.3 %reduce = bf16[128,4096]{1,0:T(8,128)(2,1)} reduce(bf16[128,1,4096]{2,0,1:T(8,128)(2,1)} %fusion.4, bf16[]{:T(256)} %broadcast.105), dimensions={1}, to_apply=%copy.26.reduce_sub_computation | reduce | bytes 2097154 | tf_op jit(solution)/shard_map/convert_element_type | solution.py:96
  98.8 2.6 %reshape.78 = bf16[128,2,2048]{2,1,0:T(2,128)(2,1)} reshape(bf16[128,4096]{1,0:T(8,128)(2,1)} %reduce) | data formatting | bytes 2097152
  101.4 10.1 %all-to-all-start.2 = ((bf16[128,2,2048]{2,1,0:T(2,128)(2,1)}), bf16[128,2,2048]{2,1,0:T(2,128)(2,1)}, u32[]{:S(2)}, u32[]{:S(2)}) async-start(bf16[128,2,2048]{2,1,0:T(2,128)(2,1)} %reshape.78), calls=%async_computation.2 | async-start | bytes 2097152 | tf_op jit(solution)/shard_map/all_to_all | solution.py:97
  111.6 0.1 reduce_sum.47
  111.7 0.1 select_reduce_fusion
  111.9 30.2 %all-to-all-done.2 = bf16[128,2,2048]{2,1,0:T(2,128)(2,1)} async-done(((bf16[128,2,2048]{2,1,0:T(2,128)(2,1)}), bf16[128,2,2048]{2,1,0:T(2,128)(2,1)}, u32[]{:S(2)}, u32[]{:S(2)}) %all-to-all-start.2) | async-done | bytes 1048608 | tf_op jit(solution)/shard_map/all_to_all | solution.py:97
  142.0 7.5 %reshape.79 = bf16[128,1,4096]{2,1,0:T(2,128)(2,1)} reshape(bf16[128,2,2048]{2,1,0:T(2,128)(2,1)} %all-to-all-done.2) | data formatting | bytes 2097152
  149.5 3.4 %convolution_convert_fusion.1 = bf16[8,4096]{1,0:T(8,128)(2,1)} fusion(bf16[128,1,4096]{2,1,0:T(2,128)(2,1)} %reshape.79, bf16[8,128]{1,0:T(8,128)(2,1)S(1)} %select_reduce_fusion), kind=kOutput, calls=%fused_computation.3 | convolution fusion | flops 8421376 | bytes 1116160 | tf_op jit(solution)/shard_map/dot_general | solution.py:99
  (12 shorter events, 0.4 us)
Async XLA Ops:
  0.0 89.3 %copy-start = (bf16[1,384,4096]{2,1,0:T(8,128)(2,1)S(1)}, bf16[1,384,4096]{2,1,0:T(8,128)(2,1)}, u32[]{:S(2)}) copy-start(bf16[1,384,4096]{2,1,0:T(8,128)(2,1)} %param.13) | copy-start | bytes 9437188
  72.0 2.9 %collective-permute-start = (bf16[128,1,4096]{2,0,1:T(8,128)(2,1)}, bf16[128,1,4096]{2,0,1:T(8,128)(2,1)S(1)}, u32[]{:S(2)}, u32[]{:S(2)}) collective-permute-start(bf16[128,1,4096]{2,0,1:T(8,128)(2,1)} %reshape_reshape.3), channel_id=1, source_target_pairs={{0,1},{1,0},{2,3},{3,2},{4,5},{5,4},{6,7},{7,6},{8,9},{9,8},{10,11... | collective-permute-start | bytes 3145736 | tf_op jit(solution)/shard_map/ppermute | solution.py:18
  90.7 3.0 %collective-permute-start.1 = (bf16[128,1,4096]{2,0,1:T(8,128)(2,1)S(1)}, bf16[128,1,4096]{2,0,1:T(8,128)(2,1)S(1)}, u32[]{:S(2)}, u32[]{:S(2)}) collective-permute-start(bf16[128,1,4096]{2,0,1:T(8,128)(2,1)S(1)} %slice.29), channel_id=1, source_target_pairs={{0,1},{1,0},{2,3},{3,2},{4,5},{5,4},{6,7},{7,6},{8,9},{9,8},{10,11... | collective-permute-start | bytes 3145736 | tf_op jit(solution)/shard_map/ppermute | solution.py:18
  98.8 12.8 %copy-start.1 = (f32[8,8]{1,0:T(8,128)S(1)}, f32[8,8]{1,0:T(8,128)}, u32[]{:S(2)}) copy-start(f32[8,8]{1,0:T(8,128)} %param.10) | copy-start | bytes 772
  101.4 40.6 %all-to-all-start.2 = ((bf16[128,2,2048]{2,1,0:T(2,128)(2,1)}), bf16[128,2,2048]{2,1,0:T(2,128)(2,1)}, u32[]{:S(2)}, u32[]{:S(2)}) async-start(bf16[128,2,2048]{2,1,0:T(2,128)(2,1)} %reshape.78), calls=%async_computation.2 | async-start | bytes 2097152 | tf_op jit(solution)/shard_map/all_to_all | solution.py:97
where the time goes:
time: 155 us; the launch traced here: 153 us
  blocking collectives  58.4 us (38%)
  waiting for transfers between devices  35.6 us (23%)
  local copies, waits for them, and re-layouts  27.2 us (18%)
  matrix products  12.2 us (8%)
  starting transfers between devices  10.5 us (7%)
  other arithmetic  8.9 us (6%)
    all_to_all x2, blocking collectives, turned_blocks(): lax.all_to_all(tiles, axes[k], split_axis=k, concat_axis=k, tiled=True)  58.4 us
    all_to_all x1, waiting for transfers between devices, on_device(): lax.all_to_all(finished, EXPERT, split_axis=0, concat_axis=0, tiled=True)  30.2 us
    unnamed x6, local copies, waits for them, and re-layouts  10.2 us
    all_to_all x1, starting transfers between devices, on_device(): lax.all_to_all(finished, EXPERT, split_axis=0, concat_axis=0, tiled=True)  10.1 us
    ppermute x2, waiting for transfers between devices, partner(): return lax.ppermute(block, axis, route)  5.4 us
    dot_general x1, matrix products, on_device(): jnp.dot(both_rows.reshape(devices * 2 * slot_count, width), w_in[0], pref...  5.21 us
    convert_element_type x2, other arithmetic, on_device(): finished = (own_part + from_partner).astype(jnp.bfloat16)  4.57 us
    another operation x2, local copies, waits for them, and re-layouts, turned_blocks(): tiles = tiles.reshape(*lengths, *tiles.shape[1:])  4.35 us
  transfers between devices with their start and end apart: 3, of which 3 were waited for; matrix products, arithmetic and copies ran while one was open for 0% of the time, Pallas kernels for 0%

commit v1 on v0

v1 whole, which is shorter than its diff:
```python
import functools

import jax
import jax.numpy as jnp
from jax import lax
from jax.experimental import pallas as pl
from jax.experimental.pallas import tpu as pltpu
from jax.sharding import Mesh
from jax.sharding import PartitionSpec as P

MESH = pl.DeviceIdType.MESH
GROUPS_EXPERT = ("groups", "y", "x", "core")
SLOTS = 2
LANES = 128
HALF_LANES = 64
CHUNKS = 4
F32 = jnp.float32
BF16 = jnp.bfloat16


def across(a, b):
    return lax.dot_general(a, b, (((1,), (1,)), ((), ())), preferred_element_type=F32)


def kernel(
    n, tokens, gain, ids, score, pair, w_in, w_out, out,
    win_v, wout_v, x, meta, g, a, acc, own, other, came, done, back, sums, last,
    win_sem, wout_sem, m_send, m_recv, s1, r1, s2, r2, s3, r3, s4, r4, sa, ra, sb, rb,
):
    y, col, core = lax.axis_index("y"), lax.axis_index("x"), lax.axis_index("core")
    first = y * (1 - core) + col * core
    second = col * (1 - core) + y * core

    def at(i, j):
        return {"y": i * (1 - core) + j * core, "x": j * (1 - core) + i * core, "core": core}

    partner = {"core": 1 - core}
    count, width = tokens.shape
    half = width // 2
    w = half // CHUNKS
    block = 2 * count
    group = n * SLOTS
    rows = n * block
    slots = n * group
    units = w_out.shape[1]

    weight_copies = []
    for k in range(CHUNKS):
        for h in range(2):
            weight_copies.append(pltpu.make_async_copy(
                w_in.at[0, pl.ds(h * half + k * w, w), :], win_v.at[k, pl.ds(h * w, w), :], win_sem.at[k, h]))
    for k in range(CHUNKS):
        for h in range(2):
            weight_copies.append(pltpu.make_async_copy(
                w_out.at[0, :, pl.ds(h * half + k * w, w)], wout_v.at[k, :, pl.ds(h * w, w)], wout_sem.at[k, h]))

    barrier = pltpu.get_barrier_semaphore()
    for d in range(1, n):
        pl.semaphore_signal(barrier, inc=1, device_id=at((first + d) % n, second), device_id_type=MESH)
        pl.semaphore_signal(barrier, inc=1, device_id=at(first, (second + d) % n), device_id_type=MESH)
    pl.semaphore_signal(barrier, inc=1, device_id=partner, device_id_type=MESH)
    for copy in weight_copies:
        copy.start()

    mine = pl.ds(pl.multiple_of(first * block, block), block)
    wide = tokens[...].astype(F32)
    scale = lax.rsqrt(jnp.mean(wide * wide, axis=-1, keepdims=True) + 1e-06)
    normed = wide * scale * gain[...]
    x[mine, :] = jnp.concatenate([normed[:, :half], normed[:, half:]], axis=0).astype(BF16)

    scores = score[...]
    shares = (scores / jnp.sum(scores, axis=-1, keepdims=True)).astype(BF16).astype(F32)
    named = ids[...]
    lane = lax.broadcasted_iota(jnp.int32, (count, LANES), 1)
    table = jnp.zeros((count, LANES), F32)
    for k in range(named.shape[1]):
        table = table + jnp.where(lane == named[:, k:k + 1], 1.0, 0.0)
        table = table + jnp.where(lane == named[:, k:k + 1] + HALF_LANES, shares[:, k:k + 1], 0.0)
    place = lax.broadcasted_iota(jnp.int32, (LANES, LANES), 0)
    table = across(table.astype(BF16), jnp.where(place == pair[...], 1.0, 0.0).astype(BF16))
    row = lax.broadcasted_iota(jnp.int32, (count, LANES), 0)
    earlier = jnp.zeros((count, LANES), F32)
    for t in range(count - 1):
        earlier = earlier + jnp.where(row > t, table[t:t + 1, :], 0.0)
    table = jnp.where(lane < HALF_LANES, table * (1.0 + earlier), table)
    meta[mine, :] = jnp.concatenate([table, table], axis=0).astype(BF16)

    pl.semaphore_wait(barrier, 2 * (n - 1) + 1)

    def send_meta(d):
        return pltpu.make_async_remote_copy(
            src_ref=meta.at[mine, :], dst_ref=meta.at[mine, :], send_sem=m_send.at[d], recv_sem=m_recv.at[d],
            device_id=at((first + d) % n, second), device_id_type=MESH)

    def send_x(k, d):
        part = pl.ds(k * w, w)
        return pltpu.make_async_remote_copy(
            src_ref=x.at[mine, part], dst_ref=x.at[mine, part], send_sem=s1.at[k, d], recv_sem=r1.at[k, d],
            device_id=at((first + d) % n, second), device_id_type=MESH)

    def group_of(j):
        return pl.ds(pl.multiple_of(j * group, group), group)

    def block_of(i):
        return pl.ds(pl.multiple_of(i * block, block), block)

    def send_slots(k, d):
        to = (second + d) % n
        return pltpu.make_async_remote_copy(
            src_ref=g.at[k, group_of(to), :], dst_ref=a.at[k, group_of(second), :],
            send_sem=s2.at[k, d], recv_sem=r2.at[k, d], device_id=at(first, to), device_id_type=MESH)

    def swap_rows(k):
        return pltpu.make_async_remote_copy(
            src_ref=a.at[k, pl.ds(0, slots), :], dst_ref=a.at[k, pl.ds(slots, slots), :],
            send_sem=sa.at[k], recv_sem=ra.at[k], device_id=partner, device_id_type=MESH)

    def swap_partial(k):
        return pltpu.make_async_remote_copy(
            src_ref=other.at[k], dst_ref=came.at[k],
            send_sem=sb.at[k], recv_sem=rb.at[k], device_id=partner, device_id_type=MESH)

    def send_back(k, d):
        to = (second + d) % n
        return pltpu.make_async_remote_copy(
            src_ref=done.at[k, group_of(to), :], dst_ref=back.at[k, group_of(second), :],
            send_sem=s3.at[k, d], recv_sem=r3.at[k, d], device_id=at(first, to), device_id_type=MESH)

    def send_sums(k, d):
        to = (first + d) % n
        return pltpu.make_async_remote_copy(
            src_ref=sums.at[k, block_of(to), :], dst_ref=last.at[k, block_of(first), :],
            send_sem=s4.at[k, d], recv_sem=r4.at[k, d], device_id=at(to, second), device_id_type=MESH)

    for d in range(1, n):
        send_meta(d).start()
    for k in range(CHUNKS):
        for d in range(1, n):
            send_x(k, d).start()

    for d in range(1, n):
        send_meta(d).wait_recv()
    stride = 1 + (n - 1) * core
    start = first * (n * (1 - core) + core)
    slot_a = lax.broadcasted_iota(jnp.int32, (slots, LANES), 0)
    lane_a = lax.broadcasted_iota(jnp.int32, (slots, LANES), 1)
    station = slot_a // group * stride + start
    choose = jnp.where(lane_a == station, 1.0, 0.0).astype(BF16)
    weigh = jnp.where(lane_a == station + HALF_LANES, 1.0, 0.0).astype(BF16)
    everything = meta[...]
    slot_s = lax.broadcasted_iota(jnp.int32, (slots, rows), 0)
    row_s = lax.broadcasted_iota(jnp.int32, (slots, rows), 1)
    hit = (across(choose, everything) == (slot_s % SLOTS + 1).astype(F32)) & (
        slot_s % group // SLOTS == row_s // block)
    picks = [jnp.where(hit & (row_s % block // count == h), 1.0, 0.0).astype(BF16) for h in range(2)]
    row_t = lax.broadcasted_iota(jnp.int32, (rows, slots), 0)
    slot_t = lax.broadcasted_iota(jnp.int32, (rows, slots), 1)
    hit_t = (across(everything, choose) == (slot_t % SLOTS + 1).astype(F32)) & (
        slot_t % group // SLOTS == row_t // block)
    share_t = across(everything, weigh)
    mixes = [jnp.where(hit_t & (row_t % block // count == h), share_t, 0.0).astype(BF16) for h in range(2)]

    def pick(k):
        for d in range(1, n):
            send_x(k, d).wait_recv()
        chunk = x[:, k * w:(k + 1) * w]
        for h in range(2):
            g[k, :, h * w:(h + 1) * w] = jnp.dot(picks[h], chunk, preferred_element_type=F32).astype(BF16)
        for d in range(1, n):
            send_slots(k, d).start()
        a[k, group_of(second), :] = g[k, group_of(second), :]

    def swap(k):
        for d in range(1, n):
            send_slots(k, d).wait_recv()
        swap_rows(k).start()

    def expand(k):
        for h in range(2):
            weight_copies[2 * k + h].wait()
        swap_rows(k).wait_recv()
        product = jnp.dot(a[k], win_v[k], preferred_element_type=F32)
        if k == 0:
            acc[...] = product
        else:
            acc[...] += product

    for stage, k in in_waves((pick, swap, expand), CHUNKS):
        stage(k)

    gate = acc[:, :units]
    hidden = (gate / (1.0 + jnp.exp(-gate)) * acc[:, units:]).astype(BF16)

    def contract(k):
        for h in range(2):
            weight_copies[2 * CHUNKS + 2 * k + h].wait()
        product = jnp.dot(hidden, wout_v[k], preferred_element_type=F32)
        other[k] = product[slots:].astype(BF16)
        own[k] = product[:slots]
        swap_partial(k).start()

    def finish(k):
        swap_partial(k).wait_recv()
        done[k] = (own[k] + came[k].astype(F32)).astype(BF16)
        for d in range(1, n):
            send_back(k, d).start()
        back[k, group_of(second), :] = done[k, group_of(second), :]

    def mix(k):
        for d in range(1, n):
            send_back(k, d).wait_recv()
        total = jnp.dot(mixes[0], back[k, :, :w], preferred_element_type=F32)
        total = total + jnp.dot(mixes[1], back[k, :, w:], preferred_element_type=F32)
        sums[k] = total.astype(BF16)
        for d in range(1, n):
            send_sums(k, d).start()
        last[k, block_of(first), :] = sums[k, block_of(first), :]

    def gather(k):
        for d in range(1, n):
            send_sums(k, d).wait_recv()
        total = last[k, 0:block, :].astype(F32)
        for i in range(1, n):
            total = total + last[k, i * block:(i + 1) * block, :].astype(F32)
        for h in range(2):
            out[:, h * half + k * w:h * half + (k + 1) * w] = total[h * count:(h + 1) * count].astype(BF16)

    for stage, k in in_waves((contract, finish, mix, gather), CHUNKS):
        stage(k)

    for d in range(1, n):
        send_meta(d).wait_send()
    for k in range(CHUNKS):
        swap_rows(k).wait_send()
        swap_partial(k).wait_send()
        for d in range(1, n):
            send_x(k, d).wait_send()
            send_slots(k, d).wait_send()
            send_back(k, d).wait_send()
            send_sums(k, d).wait_send()


def in_waves(stages, chunks):
    return [
        (stages[s], wave - s)
        for wave in range(len(stages) + chunks - 1)
        for s in range(len(stages))
        if 0 <= wave - s < chunks
    ]


def on_device(tokens, norm_gain, expert_ids, route_score, expert_pair, w_in, w_out):
    n = lax.axis_size("y")
    count, width = tokens.shape
    units = w_out.shape[1]
    w = width // 2 // CHUNKS
    rows, slots = n * 2 * count, n * n * SLOTS
    pair = jnp.full((LANES,), -1, jnp.int32)
    pair = pair.at[:expert_pair.shape[0]].set(expert_pair)
    pair = pair.at[HALF_LANES:HALF_LANES + expert_pair.shape[0]].set(expert_pair + HALF_LANES)
    vmem = pl.BlockSpec(memory_space=pltpu.VMEM)
    hbm = pl.BlockSpec(memory_space=pl.ANY)
    dma = pltpu.SemaphoreType.DMA
    return pl.pallas_call(
        functools.partial(kernel, n),
        out_shape=jax.ShapeDtypeStruct((count, width), BF16),
        in_specs=[vmem] * 5 + [hbm] * 2,
        out_specs=vmem,
        scratch_shapes=[
            pltpu.VMEM((CHUNKS, 2 * w, 2 * units), BF16),
            pltpu.VMEM((CHUNKS, units, 2 * w), BF16),
            pltpu.VMEM((rows, width // 2), BF16),
            pltpu.VMEM((rows, LANES), BF16),
            pltpu.VMEM((CHUNKS, slots, 2 * w), BF16),
            pltpu.VMEM((CHUNKS, 2 * slots, 2 * w), BF16),
            pltpu.VMEM((2 * slots, 2 * units), F32),
            pltpu.VMEM((CHUNKS, slots, 2 * w), F32),
            pltpu.VMEM((CHUNKS, slots, 2 * w), BF16),
            pltpu.VMEM((CHUNKS, slots, 2 * w), BF16),
            pltpu.VMEM((CHUNKS, slots, 2 * w), BF16),
            pltpu.VMEM((CHUNKS, slots, 2 * w), BF16),
            pltpu.VMEM((CHUNKS, rows, w), BF16),
            pltpu.VMEM((CHUNKS, rows, w), BF16),
            dma((CHUNKS, 2)), dma((CHUNKS, 2)), dma((n,)), dma((n,)),
            dma((CHUNKS, n)), dma((CHUNKS, n)), dma((CHUNKS, n)), dma((CHUNKS, n)),
            dma((CHUNKS, n)), dma((CHUNKS, n)), dma((CHUNKS, n)), dma((CHUNKS, n)),
            dma((CHUNKS,)), dma((CHUNKS,)), dma((CHUNKS,)), dma((CHUNKS,)),
        ],
        compiler_params=pltpu.CompilerParams(
            collective_id=0, has_side_effects=True, vmem_limit_bytes=48 << 20
        ),
    )(
        tokens, norm_gain.reshape(1, width), expert_ids, route_score, pair.reshape(1, LANES), w_in, w_out
    )


def solution(mesh):
    split = Mesh(mesh.devices.reshape(mesh.shape["groups"], 8, 8, 2), GROUPS_EXPERT)
    placed = (
        P(GROUPS_EXPERT, None),
        P(),
        P(GROUPS_EXPERT, None),
        P(GROUPS_EXPERT, None),
        P("groups"),
        P(GROUPS_EXPERT, None, None),
        P(GROUPS_EXPERT, None, None),
    )
    return jax.shard_map(
        on_device, mesh=split, in_specs=placed, out_specs=P(GROUPS_EXPERT, None), check_vma=False
    )
```

time: 155 us -> 86.8 us (0.56)
  Pallas kernels: 0 us -> 78.3 us
  blocking collectives: 58.4 us -> 0 us
  waiting for transfers between devices: 35.6 us -> 0 us
  local copies, waits for them, and re-layouts: 27.2 us -> 6.3 us
  matrix products: 12.2 us -> 0 us
  starting transfers between devices: 10.5 us -> 0 us
  other arithmetic: 8.9 us -> 0.66 us
    pallas_call x0 -> x1, Pallas kernels: none -> 78.3 us  [on_device(): pl.pallas_call(functools.partial(kernel, n), out_shape=jax.ShapeDtypeStru...]
    all_to_all x2 -> x0, blocking collectives: 58.4 us -> none  [turned_blocks(): lax.all_to_all(tiles, axes[k], split_axis=k, concat_axis=k, tiled=True)]
    all_to_all x1 -> x0, waiting for transfers between devices: 30.2 us -> none  [on_device(): lax.all_to_all(finished, EXPERT, split_axis=0, concat_axis=0, tiled=True)]
    dot_general x4 -> x0, matrix products: 12.2 us -> none  [the longest x1 5.21 us: on_device(): jnp.dot(both_rows.reshape(devices * 2 * slot_count, width), w_in[0], pref...]
    all_to_all x1 -> x0, starting transfers between devices: 10.1 us -> none  [on_device(): lax.all_to_all(finished, EXPERT, split_axis=0, concat_axis=0, tiled=True)]
    another operation x3 -> x0, local copies, waits for them, and re-layouts: 6.62 us -> none  [the longest x2 4.35 us: turned_blocks(): tiles = tiles.reshape(*lengths, *tiles.shape[1:])]
    ppermute x2 -> x0, waiting for transfers between devices: 5.4 us -> none  [partner(): return lax.ppermute(block, axis, route)]
    convert_element_type x5 -> x0, other arithmetic: 4.84 us -> none  [the longest x2 4.57 us: on_device(): finished = (own_part + from_partner).astype(jnp.bfloat16)]
  transfers between devices with their start and end apart: 3 -> 0, of which waited for: 3 -> 0; matrix products, arithmetic and copies ran while one was open for 0% -> 0% of each run, Pallas kernels for 0% -> 0%
where the time goes in v1:
time: 86.8 us; the launch traced here: 85.3 us
  Pallas kernels  78.3 us (90%)
  local copies, waits for them, and re-layouts  6.3 us (7%)
    pallas_call x1, Pallas kernels, on_device(): pl.pallas_call(functools.partial(kernel, n), out_shape=jax.ShapeDtypeStru...  78.3 us
    unnamed x11, local copies, waits for them, and re-layouts  5.46 us

profile of v1, /device:TPU:514, one launch (start us, length us, event | category | flops | bytes accessed | tf_op | source)
XLA Modules:
  0.0 85.3 jit_solution(10427248547456577265)
XLA Ops:
  0.0 0.7 add_bitcast_fusion
  0.7 0.7 pad_bitcast_fusion
  1.3 0.2 scatter.9.pair
  1.5 0.0 copy-start
  1.5 1.9 %copy-done = bf16[1,384,4096]{2,1,0:T(8,128)(2,1)S(1)} copy-done((bf16[1,384,4096]{2,1,0:T(8,128)(2,1)S(1)}, bf16[1,384,4096]{2,1,0:T(8,128)(2,1)}, u32[]{:S(2)}) %copy-start) | copy-done | bytes 3145752
  3.4 0.0 copy-start.1
  3.4 0.8 copy-done.1
  4.2 0.0 copy-start.2
  4.2 0.7 copy-done.2
  5.0 0.0 copy-start.3
  5.0 0.7 copy-done.3
  5.6 0.0 copy-start.4
  5.7 0.7 copy-done.4
  6.3 78.3 %shard_map.73 = bf16[8,4096]{1,0:T(8,128)(2,1)S(1)} custom-call(bf16[8,4096]{1,0:T(8,128)(2,1)S(1)} %copy-done.1, f32[1,4096]{1,0:T(1,128)S(1)} %bitcast.5, s32[8,8]{1,0:T(8,128)S(1)} %copy-done.3, f32[8,8]{1,0:T(8,128)S(1)} %copy-done.4, s32[1,128]{1,0:T(1,128)S(1)} %scatter.9.pair, bf16[1,4096,768]{2,1,0:T(8,128)(2,1)} %w_in.1, ...), custom_call_target="tpu_custom_call" | custom-call | tf_op jit(solution)/shard_map/pallas_call | solution.py:264
  84.7 0.6 copy.10
Async XLA Ops:
  1.5 1.9 %copy-start = (bf16[1,384,4096]{2,1,0:T(8,128)(2,1)S(1)}, bf16[1,384,4096]{2,1,0:T(8,128)(2,1)}, u32[]{:S(2)}) copy-start(bf16[1,384,4096]{2,1,0:T(8,128)(2,1)} %w_out.1) | copy-start | bytes 9437188
  3.4 0.8 copy-start.1
  4.2 0.7 copy-start.2
  5.0 0.7 copy-start.3
  5.6 0.7 copy-start.4

commit v2 on v1

v2 whole, which is shorter than its diff:
```python
import functools

import jax
import jax.numpy as jnp
from jax import lax
from jax.experimental import pallas as pl
from jax.experimental.pallas import tpu as pltpu
from jax.sharding import Mesh
from jax.sharding import PartitionSpec as P

MESH = pl.DeviceIdType.MESH
GROUPS_EXPERT = ("groups", "y", "x", "core")
SLOTS = 2
LANES = 128
HALF_LANES = 64
CHUNKS = 2
BATCHES = 2
F32 = jnp.float32
BF16 = jnp.bfloat16


def across(a, b):
    return lax.dot_general(a, b, (((1,), (1,)), ((), ())), preferred_element_type=F32)


def near_first(n):
    return sorted(range(n), key=lambda d: (min(d, n - d), d))


def kernel(
    n, tokens_in, gain_in, ids_in, score_in, pair_in, w_in, w_out, out,
    tokens, gain, ids, score, pair,
    win_v, wout_v, x, meta, g, a, acc, own, other, came, done, back, sums, last,
    in_sem, win_sem, wout_sem, m_send, m_recv, s1, r1, s2, r2, s3, r3, s4, r4, sa, ra, sb, rb,
):
    y, col, core = lax.axis_index("y"), lax.axis_index("x"), lax.axis_index("core")
    first = y * (1 - core) + col * core
    second = col * (1 - core) + y * core

    def at(i, j):
        return {"y": i * (1 - core) + j * core, "x": j * (1 - core) + i * core, "core": core}

    partner = {"core": 1 - core}
    count, width = tokens.shape
    half = width // 2
    w = half // CHUNKS
    block = 2 * count
    dist = near_first(n)
    each = n // BATCHES
    part = each * SLOTS
    group = 2 * part
    rows = each * block
    slots = n * group
    heads = n * part
    units = w_out.shape[1]

    barrier = pltpu.get_barrier_semaphore()
    for d in range(1, n):
        pl.semaphore_signal(barrier, inc=1, device_id=at((first + d) % n, second), device_id_type=MESH)
        pl.semaphore_signal(barrier, inc=1, device_id=at(first, (second + d) % n), device_id_type=MESH)
    pl.semaphore_signal(barrier, inc=1, device_id=partner, device_id_type=MESH)
    in_copies = [
        pltpu.make_async_copy(src, dst, in_sem.at[i])
        for i, (src, dst) in enumerate(
            [(tokens_in, tokens), (gain_in, gain), (ids_in, ids), (score_in, score), (pair_in, pair)])
    ]
    for copy in in_copies:
        copy.start()
    win_copies = [[
        pltpu.make_async_copy(w_in.at[0, pl.ds(h * half + k * w, w), :], win_v.at[k, h], win_sem.at[k, h])
        for h in range(2)] for k in range(CHUNKS)]
    wout_copies = [[
        pltpu.make_async_copy(w_out.at[0, :, pl.ds(h * half + k * w, w)], wout_v.at[k, h], wout_sem.at[k, h])
        for h in range(2)] for k in range(CHUNKS)]
    for copies in win_copies + wout_copies:
        for copy in copies:
            copy.start()

    for copy in in_copies:
        copy.wait()
    wide = tokens[...].astype(F32)
    scale = lax.rsqrt(jnp.mean(wide * wide, axis=-1, keepdims=True) + 1e-06)
    normed = wide * scale * gain[...]
    x[0:block, :] = jnp.concatenate([normed[:, :half], normed[:, half:]], axis=0).astype(BF16)

    scores = score[...]
    shares = (scores / jnp.sum(scores, axis=-1, keepdims=True)).astype(BF16).astype(F32)
    named = ids[...]
    experts = pair.shape[1]
    choice = lax.broadcasted_iota(jnp.int32, (count, experts), 1)
    member = jnp.zeros((count, experts), F32)
    weight = jnp.zeros((count, experts), F32)
    for k in range(named.shape[1]):
        same = choice == named[:, k:k + 1]
        member = member + jnp.where(same, 1.0, 0.0)
        weight = weight + jnp.where(same, shares[:, k:k + 1], 0.0)
    place = lax.broadcasted_iota(jnp.int32, (LANES, experts), 0)
    table = across(member.astype(BF16), jnp.where(place == pair[...], 1.0, 0.0).astype(BF16))
    row = lax.broadcasted_iota(jnp.int32, (count, LANES), 0)
    earlier = jnp.zeros((count, LANES), F32)
    for t in range(count - 1):
        earlier = earlier + jnp.where(row > t, table[t:t + 1, :], 0.0)
    table = table * (1.0 + earlier)
    table = table + across(
        weight.astype(BF16), jnp.where(place == pair[...] + HALF_LANES, 1.0, 0.0).astype(BF16))
    meta[0:block, :] = jnp.concatenate([table, table], axis=0).astype(BF16)

    pl.semaphore_wait(barrier, 2 * (n - 1) + 1)

    def block_of(q):
        return pl.ds(q * block, block)

    def group_of(p):
        return pl.ds(p * group, group)

    def send_meta(q):
        return pltpu.make_async_remote_copy(
            src_ref=meta.at[block_of(0), :], dst_ref=meta.at[block_of(q), :],
            send_sem=m_send.at[q], recv_sem=m_recv.at[q],
            device_id=at((first + dist[q]) % n, second), device_id_type=MESH)

    def send_x(k, q):
        lanes = pl.ds(k * w, w)
        return pltpu.make_async_remote_copy(
            src_ref=x.at[block_of(0), lanes], dst_ref=x.at[block_of(q), lanes],
            send_sem=s1.at[k, q], recv_sem=r1.at[k, q],
            device_id=at((first + dist[q]) % n, second), device_id_type=MESH)

    def send_slots(b, k, p):
        return pltpu.make_async_remote_copy(
            src_ref=g.at[b, k, group_of(p), :], dst_ref=a.at[b, k, group_of(p), :],
            send_sem=s2.at[b, k, p], recv_sem=r2.at[b, k, p],
            device_id=at(first, (second + p) % n), device_id_type=MESH)

    def swap_rows(b, k):
        return pltpu.make_async_remote_copy(
            src_ref=a.at[b, k, pl.ds(0, slots), :], dst_ref=a.at[b, k, pl.ds(slots, slots), :],
            send_sem=sa.at[b, k], recv_sem=ra.at[b, k], device_id=partner, device_id_type=MESH)

    def swap_partial(b, k):
        return pltpu.make_async_remote_copy(
            src_ref=other.at[b, k], dst_ref=came.at[b, k],
            send_sem=sb.at[b, k], recv_sem=rb.at[b, k], device_id=partner, device_id_type=MESH)

    def send_back(b, k, p):
        return pltpu.make_async_remote_copy(
            src_ref=done.at[b, k, group_of(p), :], dst_ref=back.at[b, k, group_of(p), :],
            send_sem=s3.at[b, k, p], recv_sem=r3.at[b, k, p],
            device_id=at(first, (second + n - p) % n), device_id_type=MESH)

    def send_sums(k, q):
        return pltpu.make_async_remote_copy(
            src_ref=sums.at[k, block_of(q), :], dst_ref=last.at[k, block_of(q), :],
            send_sem=s4.at[k, q], recv_sem=r4.at[k, q],
            device_id=at((first + n - dist[q]) % n, second), device_id_type=MESH)

    def sources(b):
        return [q for q in range(b * each, (b + 1) * each) if q > 0]

    targets = [p for p in near_first(n) if p > 0]
    for b in range(BATCHES):
        for q in sources(b):
            send_meta(q).start()
        for k in range(CHUNKS):
            for q in sources(b):
                send_x(k, q).start()

    stride = 1 + (n - 1) * core
    start = first * (n * (1 - core) + core)
    slot_a = lax.broadcasted_iota(jnp.int32, (slots, LANES), 0)
    lane_a = lax.broadcasted_iota(jnp.int32, (slots, LANES), 1)
    station = (slot_a // group + second) % n * stride + start
    choose = jnp.where(lane_a == station, 1.0, 0.0).astype(BF16)
    weigh = jnp.where(lane_a == station + HALF_LANES, 1.0, 0.0).astype(BF16)

    def matching(slot, line):
        return (slot % part // SLOTS == line // block) & (slot % group // part == line % block // count)

    slot_s = lax.broadcasted_iota(jnp.int32, (slots, rows), 0)
    match_s = matching(slot_s, lax.broadcasted_iota(jnp.int32, (slots, rows), 1))
    rank_s = (slot_s % SLOTS + 1).astype(F32)
    slot_t = lax.broadcasted_iota(jnp.int32, (rows, slots), 1)
    match_t = matching(slot_t, lax.broadcasted_iota(jnp.int32, (rows, slots), 0))
    rank_t = (slot_t % SLOTS + 1).astype(F32)

    def rows_of(b):
        return slice(b * rows, (b + 1) * rows)

    def pick_table(b):
        for q in sources(b):
            send_meta(q).wait_recv()
        return jnp.where((across(choose, meta[rows_of(b), :]) == rank_s) & match_s, 1.0, 0.0).astype(BF16)

    def mix_table(b):
        table = meta[rows_of(b), :]
        return jnp.where((across(table, choose) == rank_t) & match_t, across(table, weigh), 0.0).astype(BF16)

    def pick(b, k, picks):
        for q in sources(b):
            send_x(k, q).wait_recv()
        chosen = jnp.dot(picks, x[rows_of(b), k * w:(k + 1) * w], preferred_element_type=F32).astype(BF16)
        g[b, k] = chosen
        a[b, k, 0:group, :] = chosen[0:group]
        for p in targets:
            send_slots(b, k, p).start()

    def swap(b, k):
        for p in targets:
            send_slots(b, k, p).wait_recv()
        swap_rows(b, k).start()

    def expand(b, k):
        swap_rows(b, k).wait_recv()
        if b == 0:
            for copy in win_copies[k]:
                copy.wait()
        both = a[b, k].astype(F32).reshape(2 * n, 2, part, w)
        product = None
        for h in range(2):
            term = jnp.dot(
                both[:, h].reshape(2 * heads, w).astype(BF16), win_v[k, h], preferred_element_type=F32)
            product = term if product is None else product + term
        if k == 0:
            acc[b] = product
        else:
            acc[b] += product

    def activate(b):
        gate = acc[b, :, :units]
        return (gate / (1.0 + jnp.exp(-gate)) * acc[b, :, units:]).astype(BF16)

    def contract(b, k, hidden):
        if b == 0:
            for copy in wout_copies[k]:
                copy.wait()
        for h in range(2):
            product = jnp.dot(hidden, wout_v[k, h], preferred_element_type=F32)
            own[b, k, h] = product[:heads]
            other[b, k, h] = product[heads:].astype(BF16)
        swap_partial(b, k).start()

    def finish(b, k):
        swap_partial(b, k).wait_recv()
        total = [(own[b, k, h] + came[b, k, h].astype(F32)).reshape(n, 1, part, w) for h in range(2)]
        final = jnp.concatenate(total, axis=1).reshape(slots, w).astype(BF16)
        done[b, k] = final
        back[b, k, 0:group, :] = final[0:group]
        for p in targets:
            send_back(b, k, p).start()

    def mix(b, k, mixes):
        for p in targets:
            send_back(b, k, p).wait_recv()
        total = jnp.dot(mixes, back[b, k], preferred_element_type=F32).astype(BF16)
        sums[k, rows_of(b), :] = total
        if b == 0:
            last[k, 0:block, :] = total[0:block]
        for q in sources(b):
            send_sums(k, q).start()

    def gather(k):
        for q in range(1, n):
            send_sums(k, q).wait_recv()
        total = last[k, 0:block, :].astype(F32)
        for q in range(1, n):
            total = total + last[k, q * block:(q + 1) * block, :].astype(F32)
        for h in range(2):
            out[:, h * half + k * w:h * half + (k + 1) * w] = total[h * count:(h + 1) * count].astype(BF16)

    chunks = range(CHUNKS)
    for b in range(BATCHES):
        picks = pick_table(b)
        for k in chunks:
            pick(b, k, picks)
    mixes = [mix_table(b) for b in range(BATCHES)]
    for b in range(BATCHES):
        for stage, k in in_waves((swap, expand), CHUNKS):
            stage(b, k)
        hidden = activate(b)
        for k in chunks:
            contract(b, k, hidden)
        for k in chunks:
            if b > 0:
                mix(b - 1, k, mixes[b - 1])
            finish(b, k)
    for k in chunks:
        mix(BATCHES - 1, k, mixes[BATCHES - 1])
    for k in chunks:
        gather(k)

    for q in range(1, n):
        send_meta(q).wait_send()
        for k in chunks:
            send_x(k, q).wait_send()
            send_sums(k, q).wait_send()
    for b in range(BATCHES):
        for k in chunks:
            swap_rows(b, k).wait_send()
            swap_partial(b, k).wait_send()
            for p in targets:
                send_slots(b, k, p).wait_send()
                send_back(b, k, p).wait_send()


def in_waves(stages, chunks):
    return [
        (stages[s], wave - s)
        for wave in range(len(stages) + chunks - 1)
        for s in range(len(stages))
        if 0 <= wave - s < chunks
    ]


def on_device(tokens, norm_gain, expert_ids, route_score, expert_pair, w_in, w_out):
    n = lax.axis_size("y")
    count, width = tokens.shape
    units = w_out.shape[1]
    w = width // 2 // CHUNKS
    rows = n * 2 * count
    heads = n * (n // BATCHES) * SLOTS
    slots = 2 * heads
    experts = expert_pair.shape[0]
    vmem = pl.BlockSpec(memory_space=pltpu.VMEM)
    hbm = pl.BlockSpec(memory_space=pl.ANY)
    dma = pltpu.SemaphoreType.DMA
    return pl.pallas_call(
        functools.partial(kernel, n),
        out_shape=jax.ShapeDtypeStruct((count, width), BF16),
        in_specs=[hbm] * 7,
        out_specs=vmem,
        scratch_shapes=[
            pltpu.VMEM((count, width), BF16),
            pltpu.VMEM((1, width), F32),
            pltpu.VMEM(expert_ids.shape, jnp.int32),
            pltpu.VMEM(route_score.shape, F32),
            pltpu.VMEM((1, experts), jnp.int32),
            pltpu.VMEM((CHUNKS, 2, w, 2 * units), BF16),
            pltpu.VMEM((CHUNKS, 2, units, w), BF16),
            pltpu.VMEM((rows, width // 2), BF16),
            pltpu.VMEM((rows, LANES), BF16),
            pltpu.VMEM((BATCHES, CHUNKS, slots, w), BF16),
            pltpu.VMEM((BATCHES, CHUNKS, 2 * slots, w), BF16),
            pltpu.VMEM((BATCHES, 2 * heads, 2 * units), F32),
            pltpu.VMEM((BATCHES, CHUNKS, 2, heads, w), F32),
            pltpu.VMEM((BATCHES, CHUNKS, 2, heads, w), BF16),
            pltpu.VMEM((BATCHES, CHUNKS, 2, heads, w), BF16),
            pltpu.VMEM((BATCHES, CHUNKS, slots, w), BF16),
            pltpu.VMEM((BATCHES, CHUNKS, slots, w), BF16),
            pltpu.VMEM((CHUNKS, rows, w), BF16),
            pltpu.VMEM((CHUNKS, rows, w), BF16),
            dma((5,)), dma((CHUNKS, 2)), dma((CHUNKS, 2)), dma((n,)), dma((n,)),
            dma((CHUNKS, n)), dma((CHUNKS, n)), dma((BATCHES, CHUNKS, n)), dma((BATCHES, CHUNKS, n)),
            dma((BATCHES, CHUNKS, n)), dma((BATCHES, CHUNKS, n)), dma((CHUNKS, n)), dma((CHUNKS, n)),
            dma((BATCHES, CHUNKS)), dma((BATCHES, CHUNKS)), dma((BATCHES, CHUNKS)), dma((BATCHES, CHUNKS)),
        ],
        compiler_params=pltpu.CompilerParams(
            collective_id=0, has_side_effects=True, vmem_limit_bytes=60 << 20
        ),
    )(
        tokens, norm_gain.reshape(1, width), expert_ids, route_score, expert_pair.reshape(1, experts), w_in, w_out
    )


def solution(mesh):
    split = Mesh(mesh.devices.reshape(mesh.shape["groups"], 8, 8, 2), GROUPS_EXPERT)
    placed = (
        P(GROUPS_EXPERT, None),
        P(),
        P(GROUPS_EXPERT, None),
        P(GROUPS_EXPERT, None),
        P("groups"),
        P(GROUPS_EXPERT, None, None),
        P(GROUPS_EXPERT, None, None),
    )
    return jax.shard_map(
        on_device, mesh=split, in_specs=placed, out_specs=P(GROUPS_EXPERT, None), check_vma=False
    )
```

time: 86.8 us -> 75.4 us (0.87)
  Pallas kernels: 78.3 us -> 73.3 us
  local copies, waits for them, and re-layouts: 6.3 us -> 1.47 us
    pallas_call x1, Pallas kernels: 78.3 us -> 73.3 us  [on_device(): pl.pallas_call(functools.partial(kernel, n), out_shape=jax.ShapeDtypeStru...]
    unnamed x11 -> x1, local copies, waits for them, and re-layouts: 5.46 us -> 1.47 us
where the time goes in v2:
time: 75.4 us; the launch traced here: 74.7 us
  Pallas kernels  73.3 us (97%)
  local copies, waits for them, and re-layouts  1.47 us (2%)
    pallas_call x1, Pallas kernels, on_device(): pl.pallas_call(functools.partial(kernel, n), out_shape=jax.ShapeDtypeStru...  73.3 us

profile of v2, /device:TPU:514, one launch (start us, length us, event | category | flops | bytes accessed | tf_op | source)
XLA Modules:
  0.0 74.7 jit_solution(4951068062799293514)
XLA Ops:
  0.0 73.3 %shard_map.73 = bf16[8,4096]{1,0:T(8,128)(2,1)} custom-call(bf16[8,4096]{1,0:T(8,128)(2,1)} %tokens_in.1, f32[1,4096]{1,0:T(1,128)} %bitcast.2, s32[8,8]{1,0:T(8,128)} %ids_in.1, f32[8,8]{1,0:T(8,128)} %score_in.1, s32[1,64]{1,0:T(1,128)} %bitcast.3, bf16[1,4096,768]{2,1,0:T(8,128)(2,1)} %w_in.1, bf16[1,384,4096]{2,1,0:T(8,128)(2,1)} %w_out.1), custom_call_target="tpu_custom_call" | custom-call | tf_op jit(solution)/shard_map/pallas_call | solution.py:326
  73.3 1.5 %copy.9 = bf16[8,4096]{1,0:T(8,128)(2,1)} copy(bf16[8,4096]{1,0:T(8,128)(2,1)} %shard_map.73) | data formatting | bytes 131072

commit v3 on v2

--- a/solution.py
+++ b/solution.py
@@ -13,7 +13,7 @@
 SLOTS = 2
 LANES = 128
 HALF_LANES = 64
-CHUNKS = 2
+CHUNKS = 4
 BATCHES = 2
 F32 = jnp.float32
 BF16 = jnp.bfloat16
@@ -21,6 +21,10 @@
 
 def across(a, b):
     return lax.dot_general(a, b, (((1,), (1,)), ((), ())), preferred_element_type=F32)
+
+
+def drain(ref, sem):
+    pltpu.make_async_copy(ref, ref, sem).wait()
 
 
 def near_first(n):
@@ -76,13 +80,15 @@
         for copy in copies:
             copy.start()
 
-    for copy in in_copies:
+    for copy in in_copies[:2]:
         copy.wait()
     wide = tokens[...].astype(F32)
     scale = lax.rsqrt(jnp.mean(wide * wide, axis=-1, keepdims=True) + 1e-06)
     normed = wide * scale * gain[...]
     x[0:block, :] = jnp.concatenate([normed[:, :half], normed[:, half:]], axis=0).astype(BF16)
 
+    for copy in in_copies[2:]:
+        copy.wait()
     scores = score[...]
     shares = (scores / jnp.sum(scores, axis=-1, keepdims=True)).astype(BF16).astype(F32)
     named = ids[...]
@@ -116,51 +122,51 @@
     def send_meta(q):
         return pltpu.make_async_remote_copy(
             src_ref=meta.at[block_of(0), :], dst_ref=meta.at[block_of(q), :],
-            send_sem=m_send.at[q], recv_sem=m_recv.at[q],
+            send_sem=m_send, recv_sem=m_recv.at[q // each],
             device_id=at((first + dist[q]) % n, second), device_id_type=MESH)
 
     def send_x(k, q):
         lanes = pl.ds(k * w, w)
         return pltpu.make_async_remote_copy(
             src_ref=x.at[block_of(0), lanes], dst_ref=x.at[block_of(q), lanes],
-            send_sem=s1.at[k, q], recv_sem=r1.at[k, q],
+            send_sem=s1, recv_sem=r1.at[q // each, k],
             device_id=at((first + dist[q]) % n, second), device_id_type=MESH)
 
     def send_slots(b, k, p):
         return pltpu.make_async_remote_copy(
             src_ref=g.at[b, k, group_of(p), :], dst_ref=a.at[b, k, group_of(p), :],
-            send_sem=s2.at[b, k, p], recv_sem=r2.at[b, k, p],
+            send_sem=s2, recv_sem=r2.at[b, k],
             device_id=at(first, (second + p) % n), device_id_type=MESH)
 
     def swap_rows(b, k):
         return pltpu.make_async_remote_copy(
             src_ref=a.at[b, k, pl.ds(0, slots), :], dst_ref=a.at[b, k, pl.ds(slots, slots), :],
-            send_sem=sa.at[b, k], recv_sem=ra.at[b, k], device_id=partner, device_id_type=MESH)
+            send_sem=sa, recv_sem=ra.at[b, k], device_id=partner, device_id_type=MESH)
 
     def swap_partial(b, k):
         return pltpu.make_async_remote_copy(
             src_ref=other.at[b, k], dst_ref=came.at[b, k],
-            send_sem=sb.at[b, k], recv_sem=rb.at[b, k], device_id=partner, device_id_type=MESH)
+            send_sem=sb, recv_sem=rb.at[b, k], device_id=partner, device_id_type=MESH)
 
     def send_back(b, k, p):
         return pltpu.make_async_remote_copy(
             src_ref=done.at[b, k, group_of(p), :], dst_ref=back.at[b, k, group_of(p), :],
-            send_sem=s3.at[b, k, p], recv_sem=r3.at[b, k, p],
+            send_sem=s3, recv_sem=r3.at[b, k],
             device_id=at(first, (second + n - p) % n), device_id_type=MESH)
 
     def send_sums(k, q):
         return pltpu.make_async_remote_copy(
             src_ref=sums.at[k, block_of(q), :], dst_ref=last.at[k, block_of(q), :],
-            send_sem=s4.at[k, q], recv_sem=r4.at[k, q],
+            send_sem=s4, recv_sem=r4.at[k],
             device_id=at((first + n - dist[q]) % n, second), device_id_type=MESH)
 
     def sources(b):
         return [q for q in range(b * each, (b + 1) * each) if q > 0]
 
     targets = [p for p in near_first(n) if p > 0]
+    for q in range(1, n):
+        send_meta(q).start()
     for b in range(BATCHES):
-        for q in sources(b):
-            send_meta(q).start()
         for k in range(CHUNKS):
             for q in sources(b):
                 send_x(k, q).start()
@@ -186,9 +192,14 @@
     def rows_of(b):
         return slice(b * rows, (b + 1) * rows)
 
+    def far_rows(b):
+        low = max(b * rows, block)
+        return pl.ds(low, (b + 1) * rows - low)
+
+    others = pl.ds(group, slots - group)
+
     def pick_table(b):
-        for q in sources(b):
-            send_meta(q).wait_recv()
+        drain(meta.at[far_rows(b), :], m_recv.at[b])
         return jnp.where((across(choose, meta[rows_of(b), :]) == rank_s) & match_s, 1.0, 0.0).astype(BF16)
 
     def mix_table(b):
@@ -196,8 +207,7 @@
         return jnp.where((across(table, choose) == rank_t) & match_t, across(table, weigh), 0.0).astype(BF16)
 
     def pick(b, k, picks):
-        for q in sources(b):
-            send_x(k, q).wait_recv()
+        drain(x.at[far_rows(b), pl.ds(k * w, w)], r1.at[b, k])
         chosen = jnp.dot(picks, x[rows_of(b), k * w:(k + 1) * w], preferred_element_type=F32).astype(BF16)
         g[b, k] = chosen
         a[b, k, 0:group, :] = chosen[0:group]
@@ -205,8 +215,7 @@
             send_slots(b, k, p).start()
 
     def swap(b, k):
-        for p in targets:
-            send_slots(b, k, p).wait_recv()
+        drain(a.at[b, k, others, :], r2.at[b, k])
         swap_rows(b, k).start()
 
     def expand(b, k):
@@ -249,8 +258,7 @@
             send_back(b, k, p).start()
 
     def mix(b, k, mixes):
-        for p in targets:
-            send_back(b, k, p).wait_recv()
+        drain(back.at[b, k, others, :], r3.at[b, k])
         total = jnp.dot(mixes, back[b, k], preferred_element_type=F32).astype(BF16)
         sums[k, rows_of(b), :] = total
         if b == 0:
@@ -259,8 +267,7 @@
             send_sums(k, q).start()
 
     def gather(k):
-        for q in range(1, n):
-            send_sums(k, q).wait_recv()
+        drain(last.at[k, pl.ds(block, (n - 1) * block), :], r4.at[k])
         total = last[k, 0:block, :].astype(F32)
         for q in range(1, n):
             total = total + last[k, q * block:(q + 1) * block, :].astype(F32)
@@ -274,41 +281,29 @@
             pick(b, k, picks)
     mixes = [mix_table(b) for b in range(BATCHES)]
     for b in range(BATCHES):
-        for stage, k in in_waves((swap, expand), CHUNKS):
-            stage(b, k)
+        for k in chunks:
+            swap(b, k)
+        for k in chunks:
+            expand(b, k)
         hidden = activate(b)
         for k in chunks:
             contract(b, k, hidden)
         for k in chunks:
-            if b > 0:
-                mix(b - 1, k, mixes[b - 1])
             finish(b, k)
-    for k in chunks:
-        mix(BATCHES - 1, k, mixes[BATCHES - 1])
+    for b in range(BATCHES):
+        for k in chunks:
+            mix(b, k, mixes[b])
     for k in chunks:
         gather(k)
 
-    for q in range(1, n):
-        send_meta(q).wait_send()
-        for k in chunks:
-            send_x(k, q).wait_send()
-            send_sums(k, q).wait_send()
-    for b in range(BATCHES):
-        for k in chunks:
-            swap_rows(b, k).wait_send()
-            swap_partial(b, k).wait_send()
-            for p in targets:
-                send_slots(b, k, p).wait_send()
-                send_back(b, k, p).wait_send()
-
-
-def in_waves(stages, chunks):
-    return [
-        (stages[s], wave - s)
-        for wave in range(len(stages) + chunks - 1)
-        for s in range(len(stages))
-        if 0 <= wave - s < chunks
-    ]
+    blocks = pl.ds(block, (n - 1) * block)
+    drain(meta.at[blocks, :], m_send)
+    drain(x.at[blocks, :], s1)
+    drain(g.at[:, :, others, :], s2)
+    drain(a.at[:, :, pl.ds(0, slots), :], sa)
+    drain(other, sb)
+    drain(done.at[:, :, others, :], s3)
+    drain(sums.at[:, blocks, :], s4)
 
 
 def on_device(tokens, norm_gain, expert_ids, route_score, expert_pair, w_in, w_out):
@@ -348,10 +343,9 @@
             pltpu.VMEM((BATCHES, CHUNKS, slots, w), BF16),
             pltpu.VMEM((CHUNKS, rows, w), BF16),
             pltpu.VMEM((CHUNKS, rows, w), BF16),
-            dma((5,)), dma((CHUNKS, 2)), dma((CHUNKS, 2)), dma((n,)), dma((n,)),
-            dma((CHUNKS, n)), dma((CHUNKS, n)), dma((BATCHES, CHUNKS, n)), dma((BATCHES, CHUNKS, n)),
-            dma((BATCHES, CHUNKS, n)), dma((BATCHES, CHUNKS, n)), dma((CHUNKS, n)), dma((CHUNKS, n)),
-            dma((BATCHES, CHUNKS)), dma((BATCHES, CHUNKS)), dma((BATCHES, CHUNKS)), dma((BATCHES, CHUNKS)),
+            dma((5,)), dma((CHUNKS, 2)), dma((CHUNKS, 2)), dma, dma((BATCHES,)),
+            dma, dma((BATCHES, CHUNKS)), dma, dma((BATCHES, CHUNKS)), dma, dma((BATCHES, CHUNKS)), dma, dma((CHUNKS,)),
+            dma, dma((BATCHES, CHUNKS)), dma, dma((BATCHES, CHUNKS)),
         ],
         compiler_params=pltpu.CompilerParams(
             collective_id=0, has_side_effects=True, vmem_limit_bytes=60 << 20

time: 75.4 us -> 70.5 us (0.935)
  Pallas kernels: 73.3 us -> 68.8 us
    pallas_call x1, Pallas kernels: 73.3 us -> 68.8 us  [on_device(): pl.pallas_call(functools.partial(kernel, n), out_shape=jax.ShapeDtypeStru...]
where the time goes in v3:
time: 70.5 us; the launch traced here: 70.3 us
  Pallas kernels  68.8 us (98%)
  local copies, waits for them, and re-layouts  1.47 us (2%)
    pallas_call x1, Pallas kernels, on_device(): pl.pallas_call(functools.partial(kernel, n), out_shape=jax.ShapeDtypeStru...  68.8 us
    unnamed x1, local copies, waits for them, and re-layouts  1.47 us

profile of v3, /device:TPU:514, one launch (start us, length us, event | category | flops | bytes accessed | tf_op | source)
XLA Modules:
  0.0 70.3 jit_solution(4333715334474655925)
XLA Ops:
  0.0 68.8 %shard_map.73 = bf16[8,4096]{1,0:T(8,128)(2,1)} custom-call(bf16[8,4096]{1,0:T(8,128)(2,1)} %tokens_in.1, f32[1,4096]{1,0:T(1,128)} %bitcast.2, s32[8,8]{1,0:T(8,128)} %ids_in.1, f32[8,8]{1,0:T(8,128)} %score_in.1, s32[1,64]{1,0:T(1,128)} %bitcast.3, bf16[1,4096,768]{2,1,0:T(8,128)(2,1)} %w_in.1, bf16[1,384,4096]{2,1,0:T(8,128)(2,1)} %w_out.1), custom_call_target="tpu_custom_call" | custom-call | tf_op jit(solution)/shard_map/pallas_call | solution.py:321
  68.8 1.5 %copy.9 = bf16[8,4096]{1,0:T(8,128)(2,1)} copy(bf16[8,4096]{1,0:T(8,128)(2,1)} %shard_map.73) | data formatting | bytes 131072

commit v4 on v3

--- a/solution.py
+++ b/solution.py
@@ -15,6 +15,7 @@
 HALF_LANES = 64
 CHUNKS = 4
 BATCHES = 2
+LAG = 1
 F32 = jnp.float32
 BF16 = jnp.bfloat16
 
@@ -34,8 +35,8 @@
 def kernel(
     n, tokens_in, gain_in, ids_in, score_in, pair_in, w_in, w_out, out,
     tokens, gain, ids, score, pair,
-    win_v, wout_v, x, meta, g, a, acc, own, other, came, done, back, sums, last,
-    in_sem, win_sem, wout_sem, m_send, m_recv, s1, r1, s2, r2, s3, r3, s4, r4, sa, ra, sb, rb,
+    win_v, wout_v, x, meta, g, a, acc, own, other, came, done, back, sums, last, far, kept, high, low,
+    in_sem, win_sem, wout_sem, m_send, m_recv, s1, r1, s2, r2, s3, r3, s4, r4, sa, ra, sb, rb, s5, r5, mid_meta, mid_x,
 ):
     y, col, core = lax.axis_index("y"), lax.axis_index("x"), lax.axis_index("core")
     first = y * (1 - core) + col * core
@@ -50,6 +51,7 @@
     w = half // CHUNKS
     block = 2 * count
     dist = near_first(n)
+    me, high1, low1, high2, low2, high3, low3, anti = range(n)
     each = n // BATCHES
     part = each * SLOTS
     group = 2 * part
@@ -85,7 +87,7 @@
     wide = tokens[...].astype(F32)
     scale = lax.rsqrt(jnp.mean(wide * wide, axis=-1, keepdims=True) + 1e-06)
     normed = wide * scale * gain[...]
-    x[0:block, :] = jnp.concatenate([normed[:, :half], normed[:, half:]], axis=0).astype(BF16)
+    x[me * block:(me + 1) * block, :] = jnp.concatenate([normed[:, :half], normed[:, half:]], axis=0).astype(BF16)
 
     for copy in in_copies[2:]:
         copy.wait()
@@ -109,7 +111,7 @@
     table = table * (1.0 + earlier)
     table = table + across(
         weight.astype(BF16), jnp.where(place == pair[...] + HALF_LANES, 1.0, 0.0).astype(BF16))
-    meta[0:block, :] = jnp.concatenate([table, table], axis=0).astype(BF16)
+    meta[me * block:(me + 1) * block, :] = jnp.concatenate([table, table], axis=0).astype(BF16)
 
     pl.semaphore_wait(barrier, 2 * (n - 1) + 1)
 
@@ -119,18 +121,26 @@
     def group_of(p):
         return pl.ds(p * group, group)
 
+    def line_copy(src, dst, send_sem, recv_sem, hop):
+        return pltpu.make_async_remote_copy(
+            src_ref=src, dst_ref=dst, send_sem=send_sem, recv_sem=recv_sem,
+            device_id=at((first + n + hop) % n, second), device_id_type=MESH)
+
     def send_meta(q):
-        return pltpu.make_async_remote_copy(
-            src_ref=meta.at[block_of(0), :], dst_ref=meta.at[block_of(q), :],
-            send_sem=m_send, recv_sem=m_recv.at[q // each],
-            device_id=at((first + dist[q]) % n, second), device_id_type=MESH)
+        sem = mid_meta.at[q - high2] if q >= high2 else m_recv.at[0]
+        return line_copy(meta.at[block_of(me), :], meta.at[block_of(q), :], m_send, sem, dist[q])
+
+    def pass_meta(q, to, hop):
+        return line_copy(meta.at[block_of(q), :], meta.at[block_of(to), :], m_send, m_recv.at[1], hop)
 
     def send_x(k, q):
         lanes = pl.ds(k * w, w)
-        return pltpu.make_async_remote_copy(
-            src_ref=x.at[block_of(0), lanes], dst_ref=x.at[block_of(q), lanes],
-            send_sem=s1, recv_sem=r1.at[q // each, k],
-            device_id=at((first + dist[q]) % n, second), device_id_type=MESH)
+        sem = mid_x.at[q - high2, k] if q >= high2 else r1.at[0, k]
+        return line_copy(x.at[block_of(me), lanes], x.at[block_of(q), lanes], s1, sem, dist[q])
+
+    def pass_x(k, q, to, hop):
+        lanes = pl.ds(k * w, w)
+        return line_copy(x.at[block_of(q), lanes], x.at[block_of(to), lanes], s1, r1.at[1, k], hop)
 
     def send_slots(b, k, p):
         return pltpu.make_async_remote_copy(
@@ -154,22 +164,31 @@
             send_sem=s3, recv_sem=r3.at[b, k],
             device_id=at(first, (second + n - p) % n), device_id_type=MESH)
 
+    def send_far_sums(k, q):
+        hop = {anti: -2 if k % 2 == 0 else 2, low3: 1, high3: -1}[q]
+        return line_copy(sums.at[k, block_of(q), :], far.at[k, block_of(q - high3), :], s5, r5.at[k], hop)
+
     def send_sums(k, q):
-        return pltpu.make_async_remote_copy(
-            src_ref=sums.at[k, block_of(q), :], dst_ref=last.at[k, block_of(q), :],
-            send_sem=s4, recv_sem=r4.at[k],
-            device_id=at((first + n - dist[q]) % n, second), device_id_type=MESH)
-
-    def sources(b):
-        return [q for q in range(b * each, (b + 1) * each) if q > 0]
+        return line_copy(sums.at[k, block_of(q), :], last.at[k, block_of(q - high1), :], s4, r4.at[k], -dist[q])
 
     targets = [p for p in near_first(n) if p > 0]
-    for q in range(1, n):
+    for q in (high2, low2, high1, low1):
         send_meta(q).start()
-    for b in range(BATCHES):
+    for pair_of in ((high2, low2), (high1, low1)):
         for k in range(CHUNKS):
-            for q in sources(b):
+            for q in pair_of:
                 send_x(k, q).start()
+    drain(meta.at[block_of(high2), :], mid_meta.at[0])
+    pass_meta(high2, high3, 1).start()
+    pass_meta(high2, anti, 2).start()
+    drain(meta.at[block_of(low2), :], mid_meta.at[1])
+    pass_meta(low2, low3, -1).start()
+    for k in range(CHUNKS):
+        for q, to, step in ((high2, high3, 1), (low2, low3, -1)):
+            drain(x.at[block_of(q), pl.ds(k * w, w)], mid_x.at[q - high2, k])
+            pass_x(k, q, to, step).start()
+            if (k % 2 == 0) == (q == high2):
+                pass_x(k, q, anti, 2 * step).start()
 
     stride = 1 + (n - 1) * core
     start = first * (n * (1 - core) + core)
@@ -192,14 +211,13 @@
     def rows_of(b):
         return slice(b * rows, (b + 1) * rows)
 
-    def far_rows(b):
-        low = max(b * rows, block)
-        return pl.ds(low, (b + 1) * rows - low)
-
+    near_blocks = pl.ds(high1 * block, 2 * block)
+    far_blocks = pl.ds(high3 * block, 3 * block)
+    arriving = (near_blocks, far_blocks)
     others = pl.ds(group, slots - group)
 
     def pick_table(b):
-        drain(meta.at[far_rows(b), :], m_recv.at[b])
+        drain(meta.at[arriving[b], :], m_recv.at[b])
         return jnp.where((across(choose, meta[rows_of(b), :]) == rank_s) & match_s, 1.0, 0.0).astype(BF16)
 
     def mix_table(b):
@@ -207,7 +225,7 @@
         return jnp.where((across(table, choose) == rank_t) & match_t, across(table, weigh), 0.0).astype(BF16)
 
     def pick(b, k, picks):
-        drain(x.at[far_rows(b), pl.ds(k * w, w)], r1.at[b, k])
+        drain(x.at[arriving[b], pl.ds(k * w, w)], r1.at[b, k])
         chosen = jnp.dot(picks, x[rows_of(b), k * w:(k + 1) * w], preferred_element_type=F32).astype(BF16)
         g[b, k] = chosen
         a[b, k, 0:group, :] = chosen[0:group]
@@ -259,18 +277,38 @@
 
     def mix(b, k, mixes):
         drain(back.at[b, k, others, :], r3.at[b, k])
-        total = jnp.dot(mixes, back[b, k], preferred_element_type=F32).astype(BF16)
-        sums[k, rows_of(b), :] = total
+        total = jnp.dot(mixes, back[b, k], preferred_element_type=F32)
+        parts = [total[i * block:(i + 1) * block] for i in range(each)]
         if b == 0:
-            last[k, 0:block, :] = total[0:block]
-        for q in sources(b):
+            kept[k] = parts[me]
+            high[k] = parts[high2]
+            for q in (high1, low1):
+                sums[k, block_of(q), :] = parts[q].astype(BF16)
+                send_sums(k, q).start()
+        else:
+            low[k] = parts[low2 - each]
+            for q in (anti, high3, low3):
+                sums[k, block_of(q), :] = parts[q - each].astype(BF16)
+                send_far_sums(k, q).start()
+
+    def merge(k):
+        drain(far.at[k], r5.at[k])
+        over, under = high[k], low[k]
+        over = over + far[k, block_of(high3 - high3), :].astype(F32)
+        under = under + far[k, block_of(low3 - high3), :].astype(F32)
+        if k % 2 == 0:
+            over = over + far[k, block_of(anti - high3), :].astype(F32)
+        else:
+            under = under + far[k, block_of(anti - high3), :].astype(F32)
+        for q, value in ((high2, over), (low2, under)):
+            sums[k, block_of(q), :] = value.astype(BF16)
             send_sums(k, q).start()
 
     def gather(k):
-        drain(last.at[k, pl.ds(block, (n - 1) * block), :], r4.at[k])
-        total = last[k, 0:block, :].astype(F32)
-        for q in range(1, n):
-            total = total + last[k, q * block:(q + 1) * block, :].astype(F32)
+        drain(last.at[k], r4.at[k])
+        total = kept[k]
+        for q in range(4):
+            total = total + last[k, block_of(q), :].astype(F32)
         for h in range(2):
             out[:, h * half + k * w:h * half + (k + 1) * w] = total[h * count:(h + 1) * count].astype(BF16)
 
@@ -281,10 +319,11 @@
             pick(b, k, picks)
     mixes = [mix_table(b) for b in range(BATCHES)]
     for b in range(BATCHES):
-        for k in chunks:
-            swap(b, k)
-        for k in chunks:
-            expand(b, k)
+        for k in range(CHUNKS + LAG):
+            if k < CHUNKS:
+                swap(b, k)
+            if k >= LAG:
+                expand(b, k - LAG)
         hidden = activate(b)
         for k in chunks:
             contract(b, k, hidden)
@@ -294,16 +333,18 @@
         for k in chunks:
             mix(b, k, mixes[b])
     for k in chunks:
+        merge(k)
+    for k in chunks:
         gather(k)
 
-    blocks = pl.ds(block, (n - 1) * block)
-    drain(meta.at[blocks, :], m_send)
-    drain(x.at[blocks, :], s1)
+    drain(meta.at[pl.ds(block, (n - 1) * block), :], m_send)
+    drain(x.at[pl.ds(block, (n - 1) * block), :], s1)
     drain(g.at[:, :, others, :], s2)
     drain(a.at[:, :, pl.ds(0, slots), :], sa)
     drain(other, sb)
     drain(done.at[:, :, others, :], s3)
-    drain(sums.at[:, blocks, :], s4)
+    drain(last, s4)
+    drain(far, s5)
 
 
 def on_device(tokens, norm_gain, expert_ids, route_score, expert_pair, w_in, w_out):
@@ -311,7 +352,8 @@
     count, width = tokens.shape
     units = w_out.shape[1]
     w = width // 2 // CHUNKS
-    rows = n * 2 * count
+    block = 2 * count
+    rows = n * block
     heads = n * (n // BATCHES) * SLOTS
     slots = 2 * heads
     experts = expert_pair.shape[0]
@@ -342,10 +384,15 @@
             pltpu.VMEM((BATCHES, CHUNKS, slots, w), BF16),
             pltpu.VMEM((BATCHES, CHUNKS, slots, w), BF16),
             pltpu.VMEM((CHUNKS, rows, w), BF16),
-            pltpu.VMEM((CHUNKS, rows, w), BF16),
+            pltpu.VMEM((CHUNKS, 4 * block, w), BF16),
+            pltpu.VMEM((CHUNKS, 3 * block, w), BF16),
+            pltpu.VMEM((CHUNKS, block, w), F32),
+            pltpu.VMEM((CHUNKS, block, w), F32),
+            pltpu.VMEM((CHUNKS, block, w), F32),
             dma((5,)), dma((CHUNKS, 2)), dma((CHUNKS, 2)), dma, dma((BATCHES,)),
             dma, dma((BATCHES, CHUNKS)), dma, dma((BATCHES, CHUNKS)), dma, dma((BATCHES, CHUNKS)), dma, dma((CHUNKS,)),
             dma, dma((BATCHES, CHUNKS)), dma, dma((BATCHES, CHUNKS)),
+            dma, dma((CHUNKS,)), dma((2,)), dma((2, CHUNKS)),
         ],
         compiler_params=pltpu.CompilerParams(
             collective_id=0, has_side_effects=True, vmem_limit_bytes=60 << 20

time: 70.5 us -> 68 us (0.965)
  Pallas kernels: 68.8 us -> 66.3 us
    pallas_call x1, Pallas kernels: 68.8 us -> 66.3 us  [on_device(): pl.pallas_call(functools.partial(kernel, n), out_shape=jax.ShapeDtypeStru...]
where the time goes in v4:
time: 68 us; the launch traced here: 67.8 us
  Pallas kernels  66.3 us (98%)
  local copies, waits for them, and re-layouts  1.47 us (2%)
    pallas_call x1, Pallas kernels, on_device(): pl.pallas_call(functools.partial(kernel, n), out_shape=jax.ShapeDtypeStru...  66.3 us
    unnamed x1, local copies, waits for them, and re-layouts  1.47 us

profile of v4, /device:TPU:514, one launch (start us, length us, event | category | flops | bytes accessed | tf_op | source)
XLA Modules:
  0.0 67.8 jit_solution(3917773437554664030)
XLA Ops:
  0.0 66.3 %shard_map.73 = bf16[8,4096]{1,0:T(8,128)(2,1)} custom-call(bf16[8,4096]{1,0:T(8,128)(2,1)} %tokens_in.1, f32[1,4096]{1,0:T(1,128)} %bitcast.2, s32[8,8]{1,0:T(8,128)} %ids_in.1, f32[8,8]{1,0:T(8,128)} %score_in.1, s32[1,64]{1,0:T(1,128)} %bitcast.3, bf16[1,4096,768]{2,1,0:T(8,128)(2,1)} %w_in.1, bf16[1,384,4096]{2,1,0:T(8,128)(2,1)} %w_out.1), custom_call_target="tpu_custom_call" | custom-call | tf_op jit(solution)/shard_map/pallas_call | solution.py:363
  66.3 1.5 %copy.9 = bf16[8,4096]{1,0:T(8,128)(2,1)} copy(bf16[8,4096]{1,0:T(8,128)(2,1)} %shard_map.73) | data formatting | bytes 131072

commit v5 on v4

--- a/solution.py
+++ b/solution.py
@@ -171,19 +171,18 @@
     def send_sums(k, q):
         return line_copy(sums.at[k, block_of(q), :], last.at[k, block_of(q - high1), :], s4, r4.at[k], -dist[q])
 
-    targets = [p for p in near_first(n) if p > 0]
+    targets = [p for p in near_first(n)[::-1] if p > 0]
     for q in (high2, low2, high1, low1):
         send_meta(q).start()
-    for pair_of in ((high2, low2), (high1, low1)):
-        for k in range(CHUNKS):
-            for q in pair_of:
-                send_x(k, q).start()
+    for k in range(CHUNKS):
+        for q in (high2, low2, high1, low1):
+            send_x(k, q).start()
     drain(meta.at[block_of(high2), :], mid_meta.at[0])
     pass_meta(high2, high3, 1).start()
     pass_meta(high2, anti, 2).start()
     drain(meta.at[block_of(low2), :], mid_meta.at[1])
     pass_meta(low2, low3, -1).start()
-    for k in range(CHUNKS):
+    def relay(k):
         for q, to, step in ((high2, high3, 1), (low2, low3, -1)):
             drain(x.at[block_of(q), pl.ds(k * w, w)], mid_x.at[q - high2, k])
             pass_x(k, q, to, step).start()
@@ -316,6 +315,8 @@
     for b in range(BATCHES):
         picks = pick_table(b)
         for k in chunks:
+            if b == 0:
+                relay(k)
             pick(b, k, picks)
     mixes = [mix_table(b) for b in range(BATCHES)]
     for b in range(BATCHES):
@@ -358,7 +359,7 @@
     slots = 2 * heads
     experts = expert_pair.shape[0]
     vmem = pl.BlockSpec(memory_space=pltpu.VMEM)
-    hbm = pl.BlockSpec(memory_space=pl.ANY)
+    hbm = pl.BlockSpec(memory_space=pltpu.HBM)
     dma = pltpu.SemaphoreType.DMA
     return pl.pallas_call(
         functools.partial(kernel, n),
@@ -395,10 +396,15 @@
             dma, dma((CHUNKS,)), dma((2,)), dma((2, CHUNKS)),
         ],
         compiler_params=pltpu.CompilerParams(
-            collective_id=0, has_side_effects=True, vmem_limit_bytes=60 << 20
+            collective_id=0, has_side_effects=True, vmem_limit_bytes=40 << 20
         ),
     )(
-        tokens, norm_gain.reshape(1, width), expert_ids, route_score, expert_pair.reshape(1, experts), w_in, w_out
+        *[
+            pltpu.with_memory_space_constraint(v, pltpu.HBM)
+            for v in (
+                tokens, norm_gain.reshape(1, width), expert_ids, route_score, expert_pair.reshape(1, experts), w_in, w_out
+            )
+        ]
     )
 
 

time: 68 us -> 64.6 us (0.950)
  Pallas kernels: 66.3 us -> 63.9 us
  local copies, waits for them, and re-layouts: 1.47 us -> 0.63 us
    pallas_call x1, Pallas kernels: 66.3 us -> 63.9 us  [on_device(): pl.pallas_call(functools.partial(kernel, n), out_shape=jax.ShapeDtypeStru...]
    unnamed x1, local copies, waits for them, and re-layouts: 1.47 us -> 0.63 us
where the time goes in v5:
time: 64.6 us; the launch traced here: 64.5 us
  Pallas kernels  63.9 us (99%)
    pallas_call x1, Pallas kernels, on_device(): pl.pallas_call(functools.partial(kernel, n), out_shape=jax.ShapeDtypeStru...  63.9 us

profile of v5, /device:TPU:514, one launch (start us, length us, event | category | flops | bytes accessed | tf_op | source)
XLA Modules:
  0.0 64.5 jit_solution(3768630837876747913)
XLA Ops:
  0.0 63.9 %shard_map.73 = bf16[8,4096]{1,0:T(8,128)(2,1)S(1)} custom-call(bf16[8,4096]{1,0:T(8,128)(2,1)} %tokens_in.1, f32[1,4096]{1,0:T(1,128)} %bitcast.2, s32[8,8]{1,0:T(8,128)} %ids_in.1, f32[8,8]{1,0:T(8,128)} %score_in.1, s32[1,64]{1,0:T(1,128)} %bitcast.3, bf16[1,4096,768]{2,1,0:T(8,128)(2,1)} %w_in.1, bf16[1,384,4096]{2,1,0:T(8,128)(2,1)} %w_out.1), custom_call_target="tpu_custom_call" | custom-call | tf_op jit(solution)/shard_map/pallas_call | solution.py:364
  63.9 0.6 copy.9
